TPU v7x, 256 devices: a whole 4x4x8 slice. The times are simulated.
256 devices in a mesh: dp: 8 (over z), task: 16 (over y, x), mp: 2 (over core).
Axes of the slice: x: 4, y: 4, z: 8, core: 2. Of those that a mesh axis runs over, the one named last changes fastest.
Arguments:
- deltas: bfloat16 [16, 2, 256, 28672], P('task', None, 'dp', 'mp'), may hold values from -3.984375 to 3.984375, as said below
- keep_blocks: int32 [16, 2, 2], P('task'), may hold values 0 or 1
- base_weights: bfloat16 [2, 256, 28672], P(None, 'dp', 'mp'), may hold values from -6 to 6
Outputs:
- merged: float32 [2, 256, 28672], P(None, 'dp', 'mp')
Inputs may be any that keep to these rules, and one draw needn't show every extreme that they name: `deltas`: every entry is a whole multiple of 1/64.
All inputs are finite; a program needn't handle non-finite values. No bound on the sum of `keep_blocks` on one device may be relied on, other than what follows from the above.
Results may differ from a plain program's by a relative error of at most 0.0003.
Values may be sent and summed in bfloat16 or wider, within the bound.
A program may use at most 128 MiB of HBM per device.

v0:
```python
import jax
import jax.numpy as jnp
from jax import lax
from jax.sharding import PartitionSpec as P

BLOCK = 128


def in_blocks(value, dim, devices):
    lengths = value.shape
    pieces = value.reshape(*lengths[:dim], devices, lengths[dim] // devices, *lengths[dim + 1 :])
    return jnp.moveaxis(pieces, dim, 0)


def cut_rows(length, count):
    unit = 8 if length >= 8 * count else 1
    return [length // unit * k // count * unit for k in range(1, count)]


def laid_out(pieces, dim):
    lengths = list(pieces.shape[1:])
    lengths[dim] *= pieces.shape[0]
    return jnp.moveaxis(pieces, 0, dim).reshape(lengths)


def exchange_in_pieces(value, axis, pieces, split_dim, concat_dim):
    blocks = in_blocks(value, split_dim, lax.axis_size(axis))
    widest = max(range(1, max(2, blocks.ndim - 1)), key=lambda d: blocks.shape[d])
    finished = []
    for slab in jnp.split(blocks, cut_rows(blocks.shape[widest], pieces), axis=widest):
        if slab.size:
            finished.append(lax.all_to_all(slab, axis, split_axis=0, concat_axis=0, tiled=True))
    return laid_out(jnp.concatenate(finished, axis=widest), concat_dim)


def combine(totals, own_base):
    upward, downward, up_count, down_count = totals
    elected = jnp.sign(upward + downward)
    upper_mean = upward / jnp.maximum(up_count, 1.0)
    lower_mean = downward / jnp.maximum(down_count, 1.0)
    agreed = jnp.where(elected > 0, upper_mean, jnp.where(elected < 0, lower_mean, 0.0))
    return own_base.astype(jnp.float32) + agreed


def statistics(trimmed):
    upward = jnp.maximum(trimmed, 0.0)
    downward = jnp.minimum(trimmed, 0.0)
    up_count = (trimmed > 0).astype(jnp.float32)
    down_count = (trimmed < 0).astype(jnp.float32)
    return (upward, downward, up_count, down_count)


def on_device(deltas, keep_blocks, base_weights):
    row_count = deltas.shape[2]
    block_count = keep_blocks.shape[2]
    row_start = lax.axis_index("dp") * row_count
    block_of_row = (row_start + jnp.arange(row_count, dtype=jnp.int32)) // BLOCK
    block_hits = (
        block_of_row[:, None] == jnp.arange(block_count, dtype=jnp.int32)[None, :]
    ).astype(jnp.float32)
    row_keep = jnp.dot(keep_blocks[0].astype(jnp.float32), block_hits.T)
    trimmed = deltas[0].astype(jnp.float32) * row_keep[:, :, None]
    share_rows = row_count // lax.axis_size("task")
    sendable = trimmed.astype(jnp.bfloat16)[None]
    arrived = exchange_in_pieces(sendable, "task", 2, 2, 0)
    upward, downward, up_count, down_count = statistics(arrived.astype(jnp.float32))
    totals = (
        jnp.sum(upward, axis=0),
        jnp.sum(downward, axis=0),
        jnp.sum(up_count, axis=0),
        jnp.sum(down_count, axis=0),
    )
    own_base = lax.dynamic_slice_in_dim(
        base_weights, lax.axis_index("task") * share_rows, share_rows, 1
    )
    merged_part = combine(totals, own_base)
    return lax.all_gather(merged_part, "task", axis=1, tiled=True)


def solution(mesh):
    in_specs = (P("task", None, "dp", "mp"), P("task", None, None), P(None, "dp", "mp"))
    out_specs = P(None, "dp", "mp")
    return jax.shard_map(
        on_device, mesh=mesh, in_specs=in_specs, out_specs=out_specs, check_vma=False
    )
```

profile of v0, /device:TPU:32, one launch (start us, length us, event | category | flops | bytes accessed | tf_op | source)
XLA Modules:
  0.0 137.2 jit_solution(14409906547524525671)
XLA Ops:
  6.5 0.9 convolution_bitcast_fusion
  7.4 0.1 copy.19
  7.5 3.4 %copy.13 = f32[1,2,32,14336]{3,1,2,0:T(2,128)S(1)} copy(bf16[1,2,32,14336]{3,2,1,0:T(8,128)(2,1)} %param.3) | data formatting | bytes 5505024 | tf_op jit(solution)/shard_map/convert_element_type | solution.py:62
  10.9 1.6 %fusion.4 = bf16[16,1,2,2,14336]{4,2,3,0,1:T(2,128)(2,1)S(1)} fusion(f32[1,2,16,2,14336]{4,1,3,2,0:T(2,128)S(1)} %bitcast.9, f32[2,16,2]{0,2,1:T(2,128)S(1)} %bitcast.10), kind=kLoop, calls=%fused_computation.9 | loop fusion | flops 1835008 | bytes 5505280 | tf_op jit(solution)/shard_map/transpose | solution.py:12
  12.5 3.9 %fusion.8 = (bf16[16,1,1,2,14336]{4,2,3,0,1:T(2,128)(2,1)S(1)}, bf16[16,1,1,2,14336]{4,2,3,0,1:T(2,128)(2,1)S(1)}) fusion(bf16[16,1,2,2,14336]{4,2,3,0,1:T(2,128)(2,1)S(1)} %fusion.4), kind=kLoop, calls=%fused_computation.24 | loop fusion | bytes 3670016 | tf_op jit(solution)/shard_map/split | solution.py:30
  16.4 1.9 %copy.15 = bf16[16,1,1,2,14336]{4,3,2,1,0:T(2,128)(2,1)} copy(bf16[16,1,1,2,14336]{4,2,3,0,1:T(2,128)(2,1)S(1)} %get-tuple-element.9) | data formatting | bytes 1835008 | tf_op jit(solution)/shard_map/split | solution.py:30
  18.3 7.0 %all-to-all-start = ((bf16[16,1,1,2,14336]{4,3,2,1,0:T(2,128)(2,1)}), bf16[16,1,1,2,14336]{4,3,2,1,0:T(2,128)(2,1)S(1)}, u32[]{:S(2)}, u32[]{:S(2)}) async-start(bf16[16,1,1,2,14336]{4,3,2,1,0:T(2,128)(2,1)} %copy.15), calls=%async_computation | async-start | bytes 1835008 | tf_op jit(solution)/shard_map/all_to_all | solution.py:32
  25.4 1.9 %copy.16 = bf16[16,1,1,2,14336]{4,3,2,1,0:T(2,128)(2,1)} copy(bf16[16,1,1,2,14336]{4,2,3,0,1:T(2,128)(2,1)S(1)} %get-tuple-element.10) | data formatting | bytes 1835008 | tf_op jit(solution)/shard_map/split | solution.py:30
  27.2 14.2 %all-to-all-done = bf16[16,1,1,2,14336]{4,3,2,1,0:T(2,128)(2,1)S(1)} async-done(((bf16[16,1,1,2,14336]{4,3,2,1,0:T(2,128)(2,1)}), bf16[16,1,1,2,14336]{4,3,2,1,0:T(2,128)(2,1)S(1)}, u32[]{:S(2)}, u32[]{:S(2)}) %all-to-all-start) | async-done | bytes 917536 | tf_op jit(solution)/shard_map/all_to_all | solution.py:32
  41.5 3.6 %all-to-all-start.1 = ((bf16[16,1,1,2,14336]{4,3,2,1,0:T(2,128)(2,1)}), bf16[16,1,1,2,14336]{4,3,2,1,0:T(2,128)(2,1)S(1)}, u32[]{:S(2)}, u32[]{:S(2)}) async-start(bf16[16,1,1,2,14336]{4,3,2,1,0:T(2,128)(2,1)} %copy.16), calls=%async_computation.1 | async-start | bytes 1835008 | tf_op jit(solution)/shard_map/all_to_all | solution.py:32
  45.1 0.2 all-gather.2.cloned.1.call-start
  45.3 14.6 %all-to-all-done.1 = bf16[16,1,1,2,14336]{4,3,2,1,0:T(2,128)(2,1)S(1)} async-done(((bf16[16,1,1,2,14336]{4,3,2,1,0:T(2,128)(2,1)}), bf16[16,1,1,2,14336]{4,3,2,1,0:T(2,128)(2,1)S(1)}, u32[]{:S(2)}, u32[]{:S(2)}) %all-to-all-start.1) | async-done | bytes 917536 | tf_op jit(solution)/shard_map/all_to_all | solution.py:32
  59.9 8.4 %fusion.2 = (f32[2,2,14336]{2,1,0:T(2,128)S(1)}, f32[2,2,14336]{2,1,0:T(2,128)S(1)}, f32[2,2,14336]{2,1,0:T(2,128)S(1)}, f32[2,2,14336]{2,1,0:T(2,128)S(1)}) fusion(bf16[16,1,1,2,14336]{4,3,2,1,0:T(2,128)(2,1)S(1)} %all-to-all-done.1, bf16[16,1,1,2,14336]{4,3,2,1,0:T(2,128)(2,1)S(1)} %all-to-all-done), kind=kLoop, calls=%fused_computation.6 | loop fusion | flops 10780672 | bytes 2752512 | tf_op jit(solution)/shard_map/reduce_sum | solution.py:70
  68.3 1.7 %convert_add_fusion = f32[2,2,14336]{2,1,0:T(2,128)S(1)} fusion(f32[2,2,14336]{2,1,0:T(2,128)S(1)} %get-tuple-element.6, f32[2,2,14336]{2,1,0:T(2,128)S(1)} %get-tuple-element.7, f32[2,2,14336]{2,1,0:T(2,128)S(1)} %get-tuple-element.8, f32[2,2,14336]{2,1,0:T(2,128)S(1)} %get-tuple-element.5, bf16[2,32,14336]{2,1,0:T(8,128)(2,1)} %param.5, s32[]{:T(128)S(6)} %select_n.20), kind=kLoop, calls=%fused_computation.15 | loop fusion | flops 688128 | bytes 1261572 | tf_op jit(solution)/shard_map/add | solution.py:42
  70.0 0.9 copy.17
  70.9 0.0 all-gather.2.cloned.1.call-update
  70.9 53.5 %all-gather.2.cloned.1.call-done = f32[2,32,14336]{2,0,1:T(2,128)} async-done(((f32[2,2,14336]{2,0,1:T(2,128)}), f32[2,32,14336]{2,0,1:T(2,128)}) %all-gather.2.cloned.1.call-update) | async-done | bytes 3670032 | tf_op jit(solution)/shard_map/all_gather | solution.py:77
  124.3 6.0 %copy.18 = f32[2,32,14336]{2,1,0:T(8,128)} copy(f32[2,32,14336]{2,0,1:T(2,128)} %all-gather.2.cloned.1.call-done) | data formatting | bytes 7340032 | tf_op jit(solution)/shard_map/all_gather | solution.py:77
  (1 shorter events, 0.0 us)
Async XLA Ops:
  18.3 23.1 %all-to-all-start = ((bf16[16,1,1,2,14336]{4,3,2,1,0:T(2,128)(2,1)}), bf16[16,1,1,2,14336]{4,3,2,1,0:T(2,128)(2,1)S(1)}, u32[]{:S(2)}, u32[]{:S(2)}) async-start(bf16[16,1,1,2,14336]{4,3,2,1,0:T(2,128)(2,1)} %copy.15), calls=%async_computation | async-start | bytes 1835008 | tf_op jit(solution)/shard_map/all_to_all | solution.py:32
  41.5 18.5 %all-to-all-start.1 = ((bf16[16,1,1,2,14336]{4,3,2,1,0:T(2,128)(2,1)}), bf16[16,1,1,2,14336]{4,3,2,1,0:T(2,128)(2,1)S(1)}, u32[]{:S(2)}, u32[]{:S(2)}) async-start(bf16[16,1,1,2,14336]{4,3,2,1,0:T(2,128)(2,1)} %copy.16), calls=%async_computation.1 | async-start | bytes 1835008 | tf_op jit(solution)/shard_map/all_to_all | solution.py:32
  45.1 79.2 %all-gather.2.cloned.1.call-start = ((), (), s32[]{:S(2)}) async-start(), calls=%async_computation.2 | async-start | bytes 3899392 | tf_op jit(solution)/shard_map/all_gather | solution.py:77
Sparse Core Ops, SparseCore 0:
  71.0 53.2 all-gather.1
where the time goes:
time: 138 us; the launch traced here: 137 us
  waiting for transfers between devices  82.3 us (60%)
  local copies, waits for them, and re-layouts  18 us (13%)
  between operations  13.5 us (10%)
  other arithmetic  11.7 us (8%)
  starting transfers between devices  10.9 us (8%)
    all_gather x1, waiting for transfers between devices, on_device(): return lax.all_gather(merged_part, 'task', axis=1, tiled=True)  53.5 us
    all_to_all x2, waiting for transfers between devices, exchange_in_pieces(): lax.all_to_all(slab, axis, split_axis=0, concat_axis=0, tiled=True)  28.8 us
    all_to_all x2, starting transfers between devices, exchange_in_pieces(): lax.all_to_all(slab, axis, split_axis=0, concat_axis=0, tiled=True)  10.7 us
    reduce_sum x1, other arithmetic, on_device(): jnp.sum(up_count, axis=0)  8.36 us
    split x3, local copies, waits for them, and re-layouts, exchange_in_pieces(): jnp.split(blocks, cut_rows(blocks.shape[widest], pieces), axis=widest)  7.63 us
    all_gather x1, local copies, waits for them, and re-layouts, on_device(): return lax.all_gather(merged_part, 'task', axis=1, tiled=True)  6 us
    convert_element_type x1, local copies, waits for them, and re-layouts, on_device(): trimmed = deltas[0].astype(jnp.float32) * row_keep[:, :, None]  3.39 us
  transfers between devices with their start and end apart: 3, of which 3 were waited for; matrix products, arithmetic and copies ran while one was open for 1% of the time, Pallas kernels for 0%

commit v1 on v0

v1 whole, which is shorter than its diff:
```python
import functools

import jax
import jax.numpy as jnp
from jax import lax
from jax.experimental import pallas as pl
from jax.experimental.pallas import tpu as pltpu
from jax.sharding import PartitionSpec as P

BLOCK = 128
SIDE = 4
TASKS = SIDE * SIDE
MESH = pl.DeviceIdType.MESH

CHUNKS = (384, 384, 128)
FAR_FIRST = (
    (2, 2), (2, 1), (1, 2), (2, 3), (3, 2), (1, 1), (3, 3), (1, 3), (3, 1),
    (0, 2), (2, 0), (0, 1), (1, 0), (0, 3), (3, 0),
)


def fraction_table(shape):
    j = lax.broadcasted_iota(jnp.int32, shape, 1)
    n = jnp.zeros(shape, jnp.int32)
    for m in range(1, 17):
        n = n + jnp.where(j >= m * (m - 1) // 2, 1, 0)
    r = j - n * (n - 1) // 2
    r = jnp.where(n == 16, 2 * r + 1, r)
    return r.astype(jnp.float32) / n.astype(jnp.float32)


def encode(upward, downward, up_count, down_count):
    total = upward + downward
    positive = total > 0.0
    amount = jnp.where(positive, upward, -downward) * 64.0
    count = jnp.where(positive, up_count, down_count) * 64.0
    n = jnp.maximum(count, 1.0)
    whole = jnp.floor(amount / n + 0.015625)
    r = amount - whole * n
    half = jnp.floor(r * 0.5)
    odd = r - 2.0 * half
    slot = n * (n - 1.0) * 0.5 + r
    slot16 = jnp.where(odd > 0.0, 120.0 + half, 28.0 + half)
    slot = jnp.where(n > 15.5, slot16, slot)
    code = whole * 128.0 + slot
    code = jnp.where(positive, code, jnp.where(total < 0.0, -code, 0.0))
    return code.astype(jnp.int32).astype(jnp.int16)


def decode(code, table):
    c = code.astype(jnp.int32)
    a = jnp.abs(c)
    whole = lax.shift_right_logical(a, 7).astype(jnp.float32)
    part = jnp.take_along_axis(table, a & 127, axis=1)
    mean = (whole + part) * 0.015625
    return jnp.where(c < 0, -mean, mean)


def kernel(chunks, keep_ref, deltas_ref, base_ref, out_ref, own, base, *scratch):
    kinds = len(chunks)
    arrived = scratch[:kinds]
    codes = scratch[kinds : 2 * kinds]
    load_sem, send_sem, recv_sem = scratch[2 * kinds :]
    rows, columns = own.shape[1], own.shape[2]
    share = columns // TASKS
    task = lax.axis_index("task")
    y, x = task // SIDE, task % SIDE
    block = lax.axis_index("dp") * rows // BLOCK

    def at(dy, dx):
        return (y + dy) % SIDE * SIDE + (x + dx) % SIDE

    loads = [
        pltpu.make_async_copy(deltas_ref.at[0, p], own.at[p], load_sem.at[p]) for p in range(2)
    ]
    base_load = pltpu.make_async_copy(base_ref, base, load_sem.at[2])
    for load in loads:
        load.start()
    base_load.start()

    barrier = pltpu.get_barrier_semaphore()
    for dy, dx in FAR_FIRST:
        pl.semaphore_signal(barrier, inc=1, device_id={"task": at(dy, dx)}, device_id_type=MESH)

    step = columns // 8
    for p in range(2):
        loads[p].wait()
        keep = keep_ref[0, p, block].astype(jnp.float32)

        @pl.loop(0, 8)
        def _(i):
            part = pl.ds(pl.multiple_of(i * step, 128), step)
            own[p, :, part] = (own[p, :, part].astype(jnp.float32) * keep).astype(jnp.bfloat16)

    pl.semaphore_wait(barrier, len(FAR_FIRST))

    sent = []

    def send(src, dst, dy, dx):
        i = len(sent)
        copy = pltpu.make_async_remote_copy(
            src_ref=src,
            dst_ref=dst,
            send_sem=send_sem.at[i],
            recv_sem=recv_sem.at[i],
            device_id={"task": at(dy, dx)},
            device_id_type=MESH,
        )
        copy.start()
        sent.append(copy)
        return copy

    starts = [sum(chunks[:k]) for k in range(kinds)]

    def lanes(of_task, k, off=0, width=None):
        start = pl.multiple_of(of_task * share + starts[k] + off, 128)
        return pl.ds(start, width or chunks[k])

    exchange = [
        [
            send(own.at[:, :, lanes(at(dy, dx), k)], arrived[k].at[i], dy, dx)
            for i, (dy, dx) in enumerate(FAR_FIRST)
        ]
        for k in range(kinds)
    ]

    def reduce(k):
        for copy in exchange[k]:
            copy.wait_recv()
        width = chunks[k]
        tile = 128
        for p in range(2):
            for off in range(0, width, tile):
                zero = jnp.zeros((rows, tile), jnp.float32)
                upward = downward = up_count = down_count = zero
                for source in range(TASKS):
                    if source < TASKS - 1:
                        value = arrived[k][source, p, :, off : off + tile]
                    else:
                        value = own[p, :, lanes(task, k, off, tile)]
                    value = value.astype(jnp.float32)
                    up, down = jnp.maximum(value, 0.0), jnp.minimum(value, 0.0)
                    upward, downward = upward + up, downward + down
                    up_count = up_count + jnp.minimum(up, 0.015625)
                    down_count = down_count - jnp.maximum(down, -0.015625)
                codes[k][p, task, :, off : off + tile] = encode(upward, downward, up_count, down_count)

    def turn(p, first, second):
        return (second, first) if p == 0 else (first, second)

    def piece(k, p, first, second):
        return codes[k].at[p, at(*turn(p, first, second))]

    def pass_on(k, p, first, second, to_first, to_second):
        ref = piece(k, p, first, second)
        return send(ref, ref, *turn(p, to_first, to_second))

    def first_stage(k):
        return [{d: pass_on(k, p, 0, 0, d, 0) for d in (1, 3, 2)} for p in range(2)]

    def second_stage(k, line, got):
        for d in (0, 3, 1, 2):
            for p in range(2):
                if d:
                    line[p][4 - d].wait_recv()
                for e in (1, 3):
                    got[p][d, e] = pass_on(k, p, d, 0, 0, e)

    def third_stage(k, got, last):
        for d, e in ((0, 1), (3, 3), (1, 1), (2, 3)):
            for p in range(2):
                got[p][d, e].wait_recv()
                last[p][d] = pass_on(k, p, d, 4 - e, 0, e)
        for d, e in ((0, 3), (3, 1), (1, 3), (2, 1)):
            for p in range(2):
                got[p][d, e].wait_recv()

    table = fraction_table((rows, 128))

    def decode_piece(k, p, first, second):
        of_task = at(*turn(p, first, second))
        for off in range(0, chunks[k], 128):
            where = lanes(of_task, k, off, 128)
            mean = decode(codes[k][p, of_task, :, off : off + 128], table)
            out_ref[p, :, where] = base[p, :, where].astype(jnp.float32) + mean

    lines, gots, lasts = [], [], []
    for k in range(kinds):
        reduce(k)
        lines.append(first_stage(k))
        gots.append([{}, {}])
        lasts.append([{}, {}])
        if k > 0:
            second_stage(k - 1, lines[k - 1], gots[k - 1])
    second_stage(kinds - 1, lines[-1], gots[-1])
    base_load.wait()
    for k in range(kinds):
        third_stage(k, gots[k], lasts[k])
        for p in range(2):
            for d in range(4):
                for e in (0, 1, 3):
                    decode_piece(k, p, d, e)
    for k in range(kinds):
        for p in range(2):
            for d in range(4):
                lasts[k][p][d].wait_recv()
                decode_piece(k, p, d, 2)
    for copy in sent:
        copy.wait_send()


def on_device(deltas, keep_blocks, base_weights):
    halves, rows, columns = base_weights.shape
    share = columns // TASKS
    assert sum(CHUNKS) == share
    copies = len(CHUNKS) * 45
    return pl.pallas_call(
        functools.partial(kernel, CHUNKS),
        out_shape=jax.ShapeDtypeStruct((halves, rows, columns), jnp.float32),
        in_specs=[
            pl.BlockSpec(memory_space=pltpu.SMEM),
            pl.BlockSpec(memory_space=pltpu.HBM),
            pl.BlockSpec(memory_space=pltpu.HBM),
        ],
        out_specs=pl.BlockSpec(memory_space=pltpu.VMEM),
        scratch_shapes=[
            pltpu.VMEM((halves, rows, columns), jnp.bfloat16),
            pltpu.VMEM((halves, rows, columns), jnp.bfloat16),
            *[pltpu.VMEM((TASKS - 1, halves, rows, width), jnp.bfloat16) for width in CHUNKS],
            *[pltpu.VMEM((halves, TASKS, rows, width), jnp.int16) for width in CHUNKS],
            pltpu.SemaphoreType.DMA((3,)),
            pltpu.SemaphoreType.DMA((copies,)),
            pltpu.SemaphoreType.DMA((copies,)),
        ],
        compiler_params=pltpu.CompilerParams(
            collective_id=0, has_side_effects=True, vmem_limit_bytes=40 * 2**20
        ),
        name="merge",
    )(keep_blocks, deltas, base_weights)


def solution(mesh):
    in_specs = (P("task", None, "dp", "mp"), P("task", None, None), P(None, "dp", "mp"))
    out_specs = P(None, "dp", "mp")
    return jax.shard_map(
        on_device, mesh=mesh, in_specs=in_specs, out_specs=out_specs, check_vma=False
    )
```

time: 138 us -> 49.8 us (0.36)
  waiting for transfers between devices: 82.3 us -> 0 us
  Pallas kernels: 0 us -> 44.2 us
  between operations: 13.5 us -> 0.01 us
  local copies, waits for them, and re-layouts: 18 us -> 5.52 us
  other arithmetic: 11.7 us -> 0 us
  starting transfers between devices: 10.9 us -> 0 us
    all_gather x1 -> x0, waiting for transfers between devices: 53.5 us -> none  [on_device(): return lax.all_gather(merged_part, 'task', axis=1, tiled=True)]
    pallas_call x0 -> x1, Pallas kernels: none -> 44.2 us  [on_device(): pl.pallas_call(functools.partial(kernel, CHUNKS), out_shape=jax.ShapeDtyp...]
    all_to_all x2 -> x0, waiting for transfers between devices: 28.8 us -> none  [exchange_in_pieces(): lax.all_to_all(slab, axis, split_axis=0, concat_axis=0, tiled=True)]
    all_to_all x2 -> x0, starting transfers between devices: 10.7 us -> none  [exchange_in_pieces(): lax.all_to_all(slab, axis, split_axis=0, concat_axis=0, tiled=True)]
    reduce_sum x1 -> x0, other arithmetic: 8.36 us -> none  [on_device(): jnp.sum(up_count, axis=0)]
    split x3 -> x0, local copies, waits for them, and re-layouts: 7.63 us -> none  [exchange_in_pieces(): jnp.split(blocks, cut_rows(blocks.shape[widest], pieces), axis=widest)]
    all_gather x1 -> x0, local copies, waits for them, and re-layouts: 6 us -> none  [on_device(): return lax.all_gather(merged_part, 'task', axis=1, tiled=True)]
    unnamed x0 -> x7, local copies, waits for them, and re-layouts: none -> 5.52 us
  transfers between devices with their start and end apart: 3 -> 0, of which waited for: 3 -> 0; matrix products, arithmetic and copies ran while one was open for 1% -> 0% of each run, Pallas kernels for 0% -> 0%
where the time goes in v1:
time: 49.8 us; the launch traced here: 49.7 us
  Pallas kernels  44.2 us (89%)
  local copies, waits for them, and re-layouts  5.52 us (11%)
    pallas_call x1, Pallas kernels, on_device(): pl.pallas_call(functools.partial(kernel, CHUNKS), out_shape=jax.ShapeDtyp...  44.2 us
    unnamed x7, local copies, waits for them, and re-layouts  5.52 us

profile of v1, /device:TPU:32, one launch (start us, length us, event | category | flops | bytes accessed | tf_op | source)
XLA Modules:
  0.0 49.7 jit_solution(13796864608980561652)
XLA Ops:
  0.0 0.0 copy-start
  0.0 1.5 %copy-done = bf16[1,2,32,14336]{3,2,1,0:T(8,128)(2,1)S(1)} copy-done((bf16[1,2,32,14336]{3,2,1,0:T(8,128)(2,1)S(1)}, bf16[1,2,32,14336]{3,2,1,0:T(8,128)(2,1)}, u32[]{:S(2)}) %copy-start) | copy-done | bytes 1835032
  1.5 0.0 copy-start.1
  1.5 1.5 %copy-done.1 = bf16[2,32,14336]{2,1,0:T(8,128)(2,1)S(1)} copy-done((bf16[2,32,14336]{2,1,0:T(8,128)(2,1)S(1)}, bf16[2,32,14336]{2,1,0:T(8,128)(2,1)}, u32[]{:S(2)}) %copy-start.1) | copy-done | bytes 1835032
  3.0 0.0 copy-start.2
  3.0 0.7 %copy-done.2 = s32[1,2,2]{2,1,0:T(2,128)S(1)} copy-done((s32[1,2,2]{2,1,0:T(2,128)S(1)}, s32[1,2,2]{2,1,0:T(2,128)}, u32[]{:S(2)}) %copy-start.2) | copy-done | bytes 40
  3.7 44.2 %merge.1 = f32[2,32,14336]{2,1,0:T(8,128)S(1)} custom-call(s32[1,2,2]{2,1,0:T(2,128)S(1)} %copy-done.2, bf16[1,2,32,14336]{3,2,1,0:T(8,128)(2,1)S(1)} %copy-done, bf16[2,32,14336]{2,1,0:T(8,128)(2,1)S(1)} %copy-done.1), custom_call_target="tpu_custom_call" | custom-call | tf_op jit(solution)/shard_map/merge/pallas_call | solution.py:217
  47.8 1.8 %copy.5 = f32[2,32,14336]{2,1,0:T(8,128)} copy(f32[2,32,14336]{2,1,0:T(8,128)S(1)} %merge.1) | data formatting | bytes 7340032
Async XLA Ops:
  0.0 1.5 %copy-start = (bf16[1,2,32,14336]{3,2,1,0:T(8,128)(2,1)S(1)}, bf16[1,2,32,14336]{3,2,1,0:T(8,128)(2,1)}, u32[]{:S(2)}) copy-start(bf16[1,2,32,14336]{3,2,1,0:T(8,128)(2,1)} %deltas_ref.1) | copy-start | bytes 5505028
  1.5 1.5 %copy-start.1 = (bf16[2,32,14336]{2,1,0:T(8,128)(2,1)S(1)}, bf16[2,32,14336]{2,1,0:T(8,128)(2,1)}, u32[]{:S(2)}) copy-start(bf16[2,32,14336]{2,1,0:T(8,128)(2,1)} %base_ref.1) | copy-start | bytes 5505028
  3.0 0.7 %copy-start.2 = (s32[1,2,2]{2,1,0:T(2,128)S(1)}, s32[1,2,2]{2,1,0:T(2,128)}, u32[]{:S(2)}) copy-start(s32[1,2,2]{2,1,0:T(2,128)} %keep_ref.1) | copy-start | bytes 52

commit v2 on v1

--- a/solution.py
+++ b/solution.py
@@ -17,6 +17,8 @@
     (2, 2), (2, 1), (1, 2), (2, 3), (3, 2), (1, 1), (3, 3), (1, 3), (3, 1),
     (0, 2), (2, 0), (0, 1), (1, 0), (0, 3), (3, 0),
 )
+
+GROUPS = 5
 
 
 def fraction_table(shape):
@@ -56,7 +58,7 @@
     return jnp.where(c < 0, -mean, mean)
 
 
-def kernel(chunks, keep_ref, deltas_ref, base_ref, out_ref, own, base, *scratch):
+def kernel(chunks, keep_hbm, deltas_ref, base_ref, out_ref, own, base, keep_ref, keep_sem, *scratch):
     kinds = len(chunks)
     arrived = scratch[:kinds]
     codes = scratch[kinds : 2 * kinds]
@@ -77,12 +79,15 @@
     for load in loads:
         load.start()
     base_load.start()
+    keep_load = pltpu.make_async_copy(keep_hbm, keep_ref, keep_sem)
+    keep_load.start()
 
     barrier = pltpu.get_barrier_semaphore()
     for dy, dx in FAR_FIRST:
         pl.semaphore_signal(barrier, inc=1, device_id={"task": at(dy, dx)}, device_id_type=MESH)
 
     step = columns // 8
+    keep_load.wait()
     for p in range(2):
         loads[p].wait()
         keep = keep_ref[0, p, block].astype(jnp.float32)
@@ -94,21 +99,19 @@
 
     pl.semaphore_wait(barrier, len(FAR_FIRST))
 
-    sent = []
-
-    def send(src, dst, dy, dx):
-        i = len(sent)
+    def send(src, dst, pair, dy, dx):
         copy = pltpu.make_async_remote_copy(
             src_ref=src,
             dst_ref=dst,
-            send_sem=send_sem.at[i],
-            recv_sem=recv_sem.at[i],
+            send_sem=pair[0],
+            recv_sem=pair[1],
             device_id={"task": at(dy, dx)},
             device_id_type=MESH,
         )
         copy.start()
-        sent.append(copy)
-        return copy
+
+    def wait(ref, sem):
+        pltpu.make_async_copy(ref, ref, sem).wait()
 
     starts = [sum(chunks[:k]) for k in range(kinds)]
 
@@ -116,17 +119,13 @@
         start = pl.multiple_of(of_task * share + starts[k] + off, 128)
         return pl.ds(start, width or chunks[k])
 
-    exchange = [
-        [
-            send(own.at[:, :, lanes(at(dy, dx), k)], arrived[k].at[i], dy, dx)
-            for i, (dy, dx) in enumerate(FAR_FIRST)
-        ]
-        for k in range(kinds)
-    ]
+    for k in range(kinds):
+        for i, (dy, dx) in enumerate(FAR_FIRST):
+            pair = (send_sem.at[k, 0], recv_sem.at[k, 0])
+            send(own.at[:, :, lanes(at(dy, dx), k)], arrived[k].at[i], pair, dy, dx)
 
     def reduce(k):
-        for copy in exchange[k]:
-            copy.wait_recv()
+        wait(arrived[k], recv_sem.at[k, 0])
         width = chunks[k]
         tile = 128
         for p in range(2):
@@ -151,29 +150,36 @@
     def piece(k, p, first, second):
         return codes[k].at[p, at(*turn(p, first, second))]
 
-    def pass_on(k, p, first, second, to_first, to_second):
+    def pass_on(k, p, group, first, second, to_first, to_second):
         ref = piece(k, p, first, second)
-        return send(ref, ref, *turn(p, to_first, to_second))
+        pair = (send_sem.at[k, 1], recv_sem.at[k, 1 + GROUPS * p + group])
+        send(ref, ref, pair, *turn(p, to_first, to_second))
+
+    def wait_pieces(k, p, group, count):
+        wait(codes[k].at[p, pl.ds(0, count)], recv_sem.at[k, 1 + GROUPS * p + group])
 
     def first_stage(k):
-        return [{d: pass_on(k, p, 0, 0, d, 0) for d in (1, 3, 2)} for p in range(2)]
-
-    def second_stage(k, line, got):
+        for p in range(2):
+            for d in (1, 3, 2):
+                pass_on(k, p, d // 2 * (3 - d), 0, 0, d, 0)
+
+    def second_stage(k):
         for d in (0, 3, 1, 2):
             for p in range(2):
-                if d:
-                    line[p][4 - d].wait_recv()
+                if d == 3:
+                    wait_pieces(k, p, 0, 2)
+                if d == 2:
+                    wait_pieces(k, p, 1, 1)
                 for e in (1, 3):
-                    got[p][d, e] = pass_on(k, p, d, 0, 0, e)
-
-    def third_stage(k, got, last):
-        for d, e in ((0, 1), (3, 3), (1, 1), (2, 3)):
-            for p in range(2):
-                got[p][d, e].wait_recv()
-                last[p][d] = pass_on(k, p, d, 4 - e, 0, e)
-        for d, e in ((0, 3), (3, 1), (1, 3), (2, 1)):
-            for p in range(2):
-                got[p][d, e].wait_recv()
+                    group = 2 if (e == 1) == (d < 2) else 3
+                    pass_on(k, p, group, d, 0, 0, e)
+
+    def third_stage(k):
+        for p in range(2):
+            wait_pieces(k, p, 2, 4)
+            for d in range(4):
+                e = 1 if d < 2 else 3
+                pass_on(k, p, 4, d, 4 - e, 0, e)
 
     table = fraction_table((rows, 128))
 
@@ -184,41 +190,43 @@
             mean = decode(codes[k][p, of_task, :, off : off + 128], table)
             out_ref[p, :, where] = base[p, :, where].astype(jnp.float32) + mean
 
-    lines, gots, lasts = [], [], []
     for k in range(kinds):
         reduce(k)
-        lines.append(first_stage(k))
-        gots.append([{}, {}])
-        lasts.append([{}, {}])
+        first_stage(k)
         if k > 0:
-            second_stage(k - 1, lines[k - 1], gots[k - 1])
-    second_stage(kinds - 1, lines[-1], gots[-1])
+            second_stage(k - 1)
+    second_stage(kinds - 1)
     base_load.wait()
     for k in range(kinds):
-        third_stage(k, gots[k], lasts[k])
-        for p in range(2):
+        third_stage(k)
+        for p in range(2):
+            wait_pieces(k, p, 3, 4)
             for d in range(4):
                 for e in (0, 1, 3):
                     decode_piece(k, p, d, e)
     for k in range(kinds):
         for p in range(2):
+            wait_pieces(k, p, 4, 4)
             for d in range(4):
-                lasts[k][p][d].wait_recv()
                 decode_piece(k, p, d, 2)
-    for copy in sent:
-        copy.wait_send()
+    for k in range(kinds):
+        wait(arrived[k], send_sem.at[k, 0])
+        wait(codes[k].at[:, pl.ds(0, TASKS - 1)], send_sem.at[k, 1])
 
 
 def on_device(deltas, keep_blocks, base_weights):
     halves, rows, columns = base_weights.shape
     share = columns // TASKS
     assert sum(CHUNKS) == share
-    copies = len(CHUNKS) * 45
+    operands = [
+        pltpu.with_memory_space_constraint(value, pltpu.HBM)
+        for value in (keep_blocks, deltas, base_weights)
+    ]
     return pl.pallas_call(
         functools.partial(kernel, CHUNKS),
         out_shape=jax.ShapeDtypeStruct((halves, rows, columns), jnp.float32),
         in_specs=[
-            pl.BlockSpec(memory_space=pltpu.SMEM),
+            pl.BlockSpec(memory_space=pltpu.HBM),
             pl.BlockSpec(memory_space=pltpu.HBM),
             pl.BlockSpec(memory_space=pltpu.HBM),
         ],
@@ -226,17 +234,19 @@
         scratch_shapes=[
             pltpu.VMEM((halves, rows, columns), jnp.bfloat16),
             pltpu.VMEM((halves, rows, columns), jnp.bfloat16),
+            pltpu.SMEM(keep_blocks.shape, jnp.int32),
+            pltpu.SemaphoreType.DMA,
             *[pltpu.VMEM((TASKS - 1, halves, rows, width), jnp.bfloat16) for width in CHUNKS],
             *[pltpu.VMEM((halves, TASKS, rows, width), jnp.int16) for width in CHUNKS],
             pltpu.SemaphoreType.DMA((3,)),
-            pltpu.SemaphoreType.DMA((copies,)),
-            pltpu.SemaphoreType.DMA((copies,)),
+            pltpu.SemaphoreType.DMA((len(CHUNKS), 2)),
+            pltpu.SemaphoreType.DMA((len(CHUNKS), 1 + 2 * GROUPS)),
         ],
         compiler_params=pltpu.CompilerParams(
             collective_id=0, has_side_effects=True, vmem_limit_bytes=40 * 2**20
         ),
         name="merge",
-    )(keep_blocks, deltas, base_weights)
+    )(*operands)
 
 
 def solution(mesh):

time: 49.8 us -> 42.8 us (0.86)
  local copies, waits for them, and re-layouts: 5.52 us -> 1.84 us
  Pallas kernels: 44.2 us -> 40.9 us
    unnamed x7 -> x1, local copies, waits for them, and re-layouts: 5.52 us -> 1.84 us
    pallas_call x1, Pallas kernels: 44.2 us -> 40.9 us  [on_device(): pl.pallas_call(functools.partial(kernel, CHUNKS), out_shape=jax.ShapeDtyp...]
where the time goes in v2:
time: 42.8 us; the launch traced here: 42.7 us
  Pallas kernels  40.9 us (96%)
  local copies, waits for them, and re-layouts  1.84 us (4%)
    pallas_call x1, Pallas kernels, on_device(): pl.pallas_call(functools.partial(kernel, CHUNKS), out_shape=jax.ShapeDtyp...  40.9 us
    unnamed x1, local copies, waits for them, and re-layouts  1.84 us

profile of v2, /device:TPU:32, one launch (start us, length us, event | category | flops | bytes accessed | tf_op | source)
XLA Modules:
  0.0 42.7 jit_solution(4612999978465845746)
XLA Ops:
  0.0 40.9 %merge.1 = f32[2,32,14336]{2,1,0:T(8,128)S(1)} custom-call(s32[1,2,2]{2,1,0:T(2,128)} %keep_hbm.1, bf16[1,2,32,14336]{3,2,1,0:T(8,128)(2,1)} %deltas_ref.1, bf16[2,32,14336]{2,1,0:T(8,128)(2,1)} %base_ref.1), custom_call_target="tpu_custom_call" | custom-call | tf_op jit(solution)/shard_map/merge/pallas_call | solution.py:225
  40.9 1.8 %copy.5 = f32[2,32,14336]{2,1,0:T(8,128)} copy(f32[2,32,14336]{2,1,0:T(8,128)S(1)} %merge.1) | data formatting | bytes 7340032

commit v3 on v2

v3 whole, which is shorter than its diff:
```python
import functools

import jax
import jax.numpy as jnp
from jax import lax
from jax.experimental import pallas as pl
from jax.experimental.pallas import tpu as pltpu
from jax.sharding import PartitionSpec as P

BLOCK = 128
SIDE = 4
TASKS = SIDE * SIDE
MESH = pl.DeviceIdType.MESH

CHUNKS = (256, 256, 256, 128)
HALF = 16
PEERS = ((0, 2), (2, 0), (0, 1), (1, 0), (0, 3), (3, 0))
SENDS, RECEIVES = 3, 9


def fraction_table(shape):
    j = lax.broadcasted_iota(jnp.int32, shape, 1)
    n = jnp.zeros(shape, jnp.int32)
    for m in range(1, 17):
        n = n + jnp.where(j >= m * (m - 1) // 2, 1, 0)
    r = j - n * (n - 1) // 2
    r = jnp.where(n == 16, 2 * r + 1, r)
    return r.astype(jnp.float32) / n.astype(jnp.float32)


def encode(upward, downward, up_count, down_count):
    total = upward + downward
    positive = total > 0.0
    amount = jnp.where(positive, upward, -downward) * 64.0
    count = jnp.where(positive, up_count, down_count) * 64.0
    n = jnp.maximum(count, 1.0)
    whole = jnp.floor(amount / n + 0.015625)
    r = amount - whole * n
    half = jnp.floor(r * 0.5)
    odd = r - 2.0 * half
    slot = n * (n - 1.0) * 0.5 + r
    slot16 = jnp.where(odd > 0.0, 120.0 + half, 28.0 + half)
    slot = jnp.where(n > 15.5, slot16, slot)
    code = whole * 128.0 + slot
    code = jnp.where(positive, code, jnp.where(total < 0.0, -code, 0.0))
    return code.astype(jnp.int32).astype(jnp.int16)


def decode(code, table):
    c = code.astype(jnp.int32)
    a = jnp.abs(c)
    whole = lax.shift_right_logical(a, 7).astype(jnp.float32)
    part = jnp.take_along_axis(table, a & 127, axis=1)
    mean = (whole + part) * 0.015625
    return jnp.where(c < 0, -mean, mean)


def tally(values, totals=None):
    for value in values:
        value = value.astype(jnp.float32)
        up, down = jnp.maximum(value, 0.0), jnp.minimum(value, 0.0)
        new = (up, down, jnp.minimum(up, 0.015625), -jnp.maximum(down, -0.015625))
        totals = new if totals is None else tuple(a + b for a, b in zip(totals, new))
    return totals


def kernel(chunks, keep_hbm, deltas_ref, base_ref, out_ref, own, base, keep_ref, load_sem, send_sem, recv_sem, *scratch):
    kinds = len(chunks)
    bundles, line, transit, direct, merged, partial, codes = (
        scratch[i * kinds : (i + 1) * kinds] for i in range(7)
    )
    rows, columns = own.shape[1], own.shape[2]
    share = columns // TASKS
    task = lax.axis_index("task")
    y, x = task // SIDE, task % SIDE
    block = lax.axis_index("dp") * rows // BLOCK
    halves = (slice(0, HALF), slice(HALF, rows))

    def at(dy, dx):
        return (y + dy) % SIDE * SIDE + (x + dx) % SIDE

    def turn(p, first, second):
        return (second, first) if p == 0 else (first, second)

    def place(p, second):
        return ((y, x)[p] + second) % SIDE

    keep_load = pltpu.make_async_copy(keep_hbm, keep_ref, load_sem.at[3])
    keep_load.start()
    loads = [
        pltpu.make_async_copy(deltas_ref.at[0, p], own.at[p], load_sem.at[p]) for p in range(2)
    ]
    base_load = pltpu.make_async_copy(base_ref, base, load_sem.at[2])
    for load in loads:
        load.start()
    base_load.start()

    barrier = pltpu.get_barrier_semaphore()
    for dy, dx in PEERS:
        pl.semaphore_signal(barrier, inc=1, device_id={"task": at(dy, dx)}, device_id_type=MESH)
    keep_load.wait()
    keeps = [keep_ref[0, p, block].astype(jnp.float32) for p in range(2)]

    def send(src, dst, k, send_slot, recv_slot, p, first, second):
        dy, dx = turn(p, first, second)
        pltpu.make_async_remote_copy(
            src_ref=src,
            dst_ref=dst,
            send_sem=send_sem.at[k, send_slot],
            recv_sem=recv_sem.at[k, recv_slot],
            device_id={"task": at(dy, dx)},
            device_id_type=MESH,
        ).start()

    def wait(ref, sem):
        pltpu.make_async_copy(ref, ref, sem).wait()

    starts = [sum(chunks[:k]) for k in range(kinds)]

    def lanes(of_task, k, off=0, width=None):
        start = pl.multiple_of(of_task * share + starts[k] + off, 128)
        return pl.ds(start, width or chunks[k])

    def trim(k):
        for d in (2, 1, 3, 0):
            for p in range(2):
                for q in range(SIDE):
                    first = ((x, y)[p] + d) % SIDE
                    of_task = q * SIDE + first if p == 0 else first * SIDE + q
                    value = own[p, :, lanes(of_task, k)].astype(jnp.float32) * keeps[p]
                    if d:
                        bundles[k][p, d - 1, q] = value.astype(jnp.bfloat16)
                    else:
                        line[k][p, 0, q] = value.astype(jnp.bfloat16)

    def send_bundles(k):
        for d in (2, 1, 3):
            for p in range(2):
                send(bundles[k].at[p, d - 1], line[k].at[p, d], k, 0, 0, p, d, 0)

    def send_transit(k):
        wait(line[k].at[:, pl.ds(1, 3)], recv_sem.at[k, 0])
        for side, e in ((0, 1), (1, 3)):
            for p in range(2):
                far = line[k].at[p, :, place(p, 2), halves[side]]
                send(far, transit[k].at[p, side], k, 1, 1, p, 0, e)

    def send_direct(k):
        for side, e in ((0, 1), (1, 3)):
            for p in range(2):
                near = line[k].at[p, :, place(p, e), halves[1 - side]]
                send(near, direct[k].at[p, side], k, 1, 2, p, 0, e)

    def merge(k):
        wait(transit[k], recv_sem.at[k, 1])
        for side, e in ((0, 1), (1, 3)):
            for p in range(2):
                for off in range(0, chunks[k], 128):
                    tile = slice(off, off + 128)
                    values = [transit[k][p, side, j, :, tile] for j in range(SIDE)]
                    values += [line[k][p, j, place(p, e), halves[side], tile] for j in range(SIDE)]
                    for i, total in enumerate(tally(values)):
                        total = (total * 64.0).astype(jnp.int32).astype(jnp.int16)
                        merged[k][p, side, i, :, tile] = total
        for side, e in ((0, 1), (1, 3)):
            for p in range(2):
                send(merged[k].at[p, side], partial[k].at[p, side], k, 1, 3, p, 0, e)

    def reduce(k):
        wait(direct[k], recv_sem.at[k, 2])
        wait(partial[k], recv_sem.at[k, 3])
        for p in range(2):
            for side in range(2):
                for off in range(0, chunks[k], 128):
                    tile = slice(off, off + 128)
                    totals = tuple(
                        partial[k][p, side, i, :, tile].astype(jnp.int32).astype(jnp.float32) * 0.015625
                        for i in range(4)
                    )
                    values = [direct[k][p, 1 - side, j, :, tile] for j in range(SIDE)]
                    values += [line[k][p, j, place(p, 0), halves[side], tile] for j in range(SIDE)]
                    codes[k][p, task, halves[side], tile] = encode(*tally(values, totals))

    def pass_on(k, p, group, first, second, to_first, to_second):
        ref = codes[k].at[p, at(*turn(p, first, second))]
        send(ref, ref, k, 2, 4 + group, p, to_first, to_second)

    def wait_codes(k, group, count):
        wait(codes[k].at[:, pl.ds(0, count)], recv_sem.at[k, 4 + group])

    def first_stage(k):
        for d in (2, 1, 3):
            for p in range(2):
                pass_on(k, p, 1 if d == 2 else 0, 0, 0, d, 0)

    def second_stage(k, d):
        for p in range(2):
            for e in (1, 3):
                group = 2 if (e == 1) == (d < 2) else 3
                pass_on(k, p, group, d, 0, 0, e)

    def third_stage(k):
        wait_codes(k, 2, 4)
        for d in range(4):
            for p in range(2):
                e = 1 if d < 2 else 3
                pass_on(k, p, 4, d, 4 - e, 0, e)

    table = fraction_table((rows, 128))

    def finish(k, seconds):
        for p in range(2):
            for d in range(4):
                for e in seconds:
                    of_task = at(*turn(p, d, e))
                    for off in range(0, chunks[k], 128):
                        where = lanes(of_task, k, off, 128)
                        mean = decode(codes[k][p, of_task, :, off : off + 128], table)
                        out_ref[p, :, where] = base[p, :, where].astype(jnp.float32) + mean

    def enter(k):
        trim(k)
        if k == 0:
            pl.semaphore_wait(barrier, len(PEERS))
        send_bundles(k)

    def own_codes(k):
        second_stage(k, 0)

    def near_codes(k):
        wait_codes(k, 0, 2)
        second_stage(k, 3)
        second_stage(k, 1)

    def far_codes(k):
        wait_codes(k, 1, 1)
        second_stage(k, 2)

    def gather(k):
        reduce(k)
        first_stage(k)

    def finish_near(k):
        if k == 0:
            base_load.wait()
        wait_codes(k, 3, 4)
        finish(k, (0, 1, 3))

    def finish_far(k):
        wait_codes(k, 4, 4)
        finish(k, (2,))

    for load in loads:
        load.wait()
    for steps in (
        (enter,), (send_transit, send_direct), (merge,), (gather, own_codes), (near_codes, far_codes),
        (third_stage,), (finish_near,), (finish_far,),
    ):
        for k in range(kinds):
            for step in steps:
                step(k)
    for k in range(kinds):
        wait(bundles[k], send_sem.at[k, 0])
        wait(bundles[k], send_sem.at[k, 1])
        wait(codes[k].at[:, pl.ds(0, TASKS - 1)], send_sem.at[k, 2])


def on_device(deltas, keep_blocks, base_weights):
    halves, rows, columns = base_weights.shape
    share = columns // TASKS
    assert sum(CHUNKS) == share
    operands = [
        pltpu.with_memory_space_constraint(value, pltpu.HBM)
        for value in (keep_blocks, deltas, base_weights)
    ]
    return pl.pallas_call(
        functools.partial(kernel, CHUNKS),
        out_shape=jax.ShapeDtypeStruct((halves, rows, columns), jnp.float32),
        in_specs=[
            pl.BlockSpec(memory_space=pltpu.HBM),
            pl.BlockSpec(memory_space=pltpu.HBM),
            pl.BlockSpec(memory_space=pltpu.HBM),
        ],
        out_specs=pl.BlockSpec(memory_space=pltpu.VMEM),
        scratch_shapes=[
            pltpu.VMEM((halves, rows, columns), jnp.bfloat16),
            pltpu.VMEM((halves, rows, columns), jnp.bfloat16),
            pltpu.SMEM(keep_blocks.shape, jnp.int32),
            pltpu.SemaphoreType.DMA((4,)),
            pltpu.SemaphoreType.DMA((len(CHUNKS), SENDS)),
            pltpu.SemaphoreType.DMA((len(CHUNKS), RECEIVES)),
            *[pltpu.VMEM((halves, SIDE - 1, SIDE, rows, width), jnp.bfloat16) for width in CHUNKS],
            *[pltpu.VMEM((halves, SIDE, SIDE, rows, width), jnp.bfloat16) for width in CHUNKS],
            *[pltpu.VMEM((halves, 2, SIDE, HALF, width), jnp.bfloat16) for width in CHUNKS * 2],
            *[pltpu.VMEM((halves, 2, 4, HALF, width), jnp.int16) for width in CHUNKS * 2],
            *[pltpu.VMEM((halves, TASKS, rows, width), jnp.int16) for width in CHUNKS],
        ],
        compiler_params=pltpu.CompilerParams(
            collective_id=0, has_side_effects=True, vmem_limit_bytes=40 * 2**20
        ),
        name="merge",
    )(*operands)


def solution(mesh):
    in_specs = (P("task", None, "dp", "mp"), P("task", None, None), P(None, "dp", "mp"))
    out_specs = P(None, "dp", "mp")
    return jax.shard_map(
        on_device, mesh=mesh, in_specs=in_specs, out_specs=out_specs, check_vma=False
    )
```

time: 42.8 us -> 38.7 us (0.904)
  Pallas kernels: 40.9 us -> 36.8 us
    pallas_call x1, Pallas kernels: 40.9 us -> 36.8 us  [on_device(): pl.pallas_call(functools.partial(kernel, CHUNKS), out_shape=jax.ShapeDtyp...]
where the time goes in v3:
time: 38.7 us; the launch traced here: 38.6 us
  Pallas kernels  36.8 us (95%)
  local copies, waits for them, and re-layouts  1.84 us (5%)
    pallas_call x1, Pallas kernels, on_device(): pl.pallas_call(functools.partial(kernel, CHUNKS), out_shape=jax.ShapeDtyp...  36.8 us
    unnamed x1, local copies, waits for them, and re-layouts  1.84 us

profile of v3, /device:TPU:32, one launch (start us, length us, event | category | flops | bytes accessed | tf_op | source)
XLA Modules:
  0.0 38.6 jit_solution(15462375595187906860)
XLA Ops:
  0.0 36.8 %merge.1 = f32[2,32,14336]{2,1,0:T(8,128)S(1)} custom-call(s32[1,2,2]{2,1,0:T(2,128)} %keep_hbm.1, bf16[1,2,32,14336]{3,2,1,0:T(8,128)(2,1)} %deltas_ref.1, bf16[2,32,14336]{2,1,0:T(8,128)(2,1)} %base_ref.1), custom_call_target="tpu_custom_call" | custom-call | tf_op jit(solution)/shard_map/merge/pallas_call | solution.py:276
  36.8 1.8 %copy.5 = f32[2,32,14336]{2,1,0:T(8,128)} copy(f32[2,32,14336]{2,1,0:T(8,128)S(1)} %merge.1) | data formatting | bytes 7340032

commit v4 on v3

--- a/solution.py
+++ b/solution.py
@@ -15,7 +15,15 @@
 CHUNKS = (256, 256, 256, 128)
 HALF = 16
 PEERS = ((0, 2), (2, 0), (0, 1), (1, 0), (0, 3), (3, 0))
-SENDS, RECEIVES = 3, 9
+SENDS, RECEIVES = 3, 8
+
+ORDER = (
+    ("A", 0), ("A", 1), ("A", 2), ("A", 3), ("B", 1), ("B", 0), ("C", 1), ("B", 2), ("C", 0), ("B", 3),
+    ("D", 1), ("D", 0), ("C", 2), ("D", 2), ("D", 3), ("C", 3), ("E", 1), ("E", 0), ("F", 0), ("F", 1),
+    ("E", 2), ("F", 2), ("E", 3), ("G", 1), ("G", 0), ("H", 1), ("H", 0), ("G", 2), ("H", 2), ("G", 3),
+    ("F", 3), ("H", 3), ("I", 1), ("J", 1), ("I", 0), ("I", 2), ("I", 3), ("J", 0), ("J", 3), ("J", 2),
+    ("K", 0), ("K", 1), ("K", 2), ("K", 3),
+)
 
 
 def fraction_table(shape):
@@ -85,15 +93,22 @@
     def place(p, second):
         return ((y, x)[p] + second) % SIDE
 
-    keep_load = pltpu.make_async_copy(keep_hbm, keep_ref, load_sem.at[3])
+    starts = [sum(chunks[:k]) for k in range(kinds)]
+
+    def lanes(of_task, k, off=0, width=None):
+        start = pl.multiple_of(TASKS * starts[k] + of_task * chunks[k] + off, 128)
+        return pl.ds(start, width or chunks[k])
+
+    loads = []
+    for k in range(kinds):
+        part = pl.ds(TASKS * starts[k], TASKS * chunks[k])
+        source, target = deltas_ref.at[0, :, :, part], own.at[:, :, part]
+        loads.append(pltpu.make_async_copy(source, target, load_sem.at[k]))
+    keep_load = pltpu.make_async_copy(keep_hbm, keep_ref, load_sem.at[kinds])
+    base_load = pltpu.make_async_copy(base_ref, base, load_sem.at[kinds + 1])
     keep_load.start()
-    loads = [
-        pltpu.make_async_copy(deltas_ref.at[0, p], own.at[p], load_sem.at[p]) for p in range(2)
-    ]
-    base_load = pltpu.make_async_copy(base_ref, base, load_sem.at[2])
     for load in loads:
         load.start()
-    base_load.start()
 
     barrier = pltpu.get_barrier_semaphore()
     for dy, dx in PEERS:
@@ -106,7 +121,7 @@
         pltpu.make_async_remote_copy(
             src_ref=src,
             dst_ref=dst,
-            send_sem=send_sem.at[k, send_slot],
+            send_sem=send_sem.at[send_slot],
             recv_sem=recv_sem.at[k, recv_slot],
             device_id={"task": at(dy, dx)},
             device_id_type=MESH,
@@ -114,12 +129,6 @@
 
     def wait(ref, sem):
         pltpu.make_async_copy(ref, ref, sem).wait()
-
-    starts = [sum(chunks[:k]) for k in range(kinds)]
-
-    def lanes(of_task, k, off=0, width=None):
-        start = pl.multiple_of(of_task * share + starts[k] + off, 128)
-        return pl.ds(start, width or chunks[k])
 
     def trim(k):
         for d in (2, 1, 3, 0):
@@ -164,11 +173,10 @@
                         merged[k][p, side, i, :, tile] = total
         for side, e in ((0, 1), (1, 3)):
             for p in range(2):
-                send(merged[k].at[p, side], partial[k].at[p, side], k, 1, 3, p, 0, e)
+                send(merged[k].at[p, side], partial[k].at[p, side], k, 1, 2, p, 0, e)
 
     def reduce(k):
-        wait(direct[k], recv_sem.at[k, 2])
-        wait(partial[k], recv_sem.at[k, 3])
+        wait(bundles[k].at[:, pl.ds(0, 2)], recv_sem.at[k, 2])
         for p in range(2):
             for side in range(2):
                 for off in range(0, chunks[k], 128):
@@ -183,10 +191,10 @@
 
     def pass_on(k, p, group, first, second, to_first, to_second):
         ref = codes[k].at[p, at(*turn(p, first, second))]
-        send(ref, ref, k, 2, 4 + group, p, to_first, to_second)
+        send(ref, ref, k, 2, 3 + group, p, to_first, to_second)
 
     def wait_codes(k, group, count):
-        wait(codes[k].at[:, pl.ds(0, count)], recv_sem.at[k, 4 + group])
+        wait(codes[k].at[:, pl.ds(0, count)], recv_sem.at[k, 3 + group])
 
     def first_stage(k):
         for d in (2, 1, 3):
@@ -219,9 +227,12 @@
                         out_ref[p, :, where] = base[p, :, where].astype(jnp.float32) + mean
 
     def enter(k):
+        loads[k].wait()
         trim(k)
         if k == 0:
             pl.semaphore_wait(barrier, len(PEERS))
+        if k == kinds - 1:
+            base_load.start()
         send_bundles(k)
 
     def own_codes(k):
@@ -241,8 +252,6 @@
         first_stage(k)
 
     def finish_near(k):
-        if k == 0:
-            base_load.wait()
         wait_codes(k, 3, 4)
         finish(k, (0, 1, 3))
 
@@ -250,19 +259,17 @@
         wait_codes(k, 4, 4)
         finish(k, (2,))
 
-    for load in loads:
-        load.wait()
-    for steps in (
-        (enter,), (send_transit, send_direct), (merge,), (gather, own_codes), (near_codes, far_codes),
-        (third_stage,), (finish_near,), (finish_far,),
-    ):
-        for k in range(kinds):
-            for step in steps:
-                step(k)
-    for k in range(kinds):
-        wait(bundles[k], send_sem.at[k, 0])
-        wait(bundles[k], send_sem.at[k, 1])
-        wait(codes[k].at[:, pl.ds(0, TASKS - 1)], send_sem.at[k, 2])
+    stages = dict(
+        A=enter, B=send_transit, C=send_direct, D=merge, E=gather, F=own_codes, G=near_codes, H=far_codes,
+        I=third_stage, J=finish_near, K=finish_far,
+    )
+    first_finish = next(k for stage, k in ORDER if stage == "J")
+    for stage, k in ORDER:
+        if (stage, k) == ("J", first_finish):
+            base_load.wait()
+        stages[stage](k)
+    for slot, pieces in ((0, TASKS - SIDE), (1, TASKS - SIDE), (2, TASKS - 1)):
+        wait(own.at[:, :, pl.ds(0, pieces * share)], send_sem.at[slot])
 
 
 def on_device(deltas, keep_blocks, base_weights):
@@ -286,8 +293,8 @@
             pltpu.VMEM((halves, rows, columns), jnp.bfloat16),
             pltpu.VMEM((halves, rows, columns), jnp.bfloat16),
             pltpu.SMEM(keep_blocks.shape, jnp.int32),
-            pltpu.SemaphoreType.DMA((4,)),
-            pltpu.SemaphoreType.DMA((len(CHUNKS), SENDS)),
+            pltpu.SemaphoreType.DMA((len(CHUNKS) + 2,)),
+            pltpu.SemaphoreType.DMA((SENDS,)),
             pltpu.SemaphoreType.DMA((len(CHUNKS), RECEIVES)),
             *[pltpu.VMEM((halves, SIDE - 1, SIDE, rows, width), jnp.bfloat16) for width in CHUNKS],
             *[pltpu.VMEM((halves, SIDE, SIDE, rows, width), jnp.bfloat16) for width in CHUNKS],

time: 38.7 us -> 38.1 us (0.984)
  Pallas kernels: 36.8 us -> 36.2 us
    pallas_call x1, Pallas kernels: 36.8 us -> 36.2 us  [on_device(): pl.pallas_call(functools.partial(kernel, CHUNKS), out_shape=jax.ShapeDtyp...]
where the time goes in v4:
time: 38.1 us
  Pallas kernels  36.2 us (95%)
  local copies, waits for them, and re-layouts  1.84 us (5%)
    pallas_call x1, Pallas kernels, on_device(): pl.pallas_call(functools.partial(kernel, CHUNKS), out_shape=jax.ShapeDtyp...  36.2 us
    unnamed x1, local copies, waits for them, and re-layouts  1.84 us

profile of v4, /device:TPU:32, one launch (start us, length us, event | category | flops | bytes accessed | tf_op | source)
XLA Modules:
  0.0 38.1 jit_solution(3028270654820661941)
XLA Ops:
  0.0 36.2 %merge.1 = f32[2,32,14336]{2,1,0:T(8,128)S(1)} custom-call(s32[1,2,2]{2,1,0:T(2,128)} %keep_hbm.1, bf16[1,2,32,14336]{3,2,1,0:T(8,128)(2,1)} %deltas_ref.1, bf16[2,32,14336]{2,1,0:T(8,128)(2,1)} %base_ref.1), custom_call_target="tpu_custom_call" | custom-call | tf_op jit(solution)/shard_map/merge/pallas_call | solution.py:283
  36.2 1.8 %copy.5 = f32[2,32,14336]{2,1,0:T(8,128)} copy(f32[2,32,14336]{2,1,0:T(8,128)S(1)} %merge.1) | data formatting | bytes 7340032

commit v5 on v4

--- a/solution.py
+++ b/solution.py
@@ -19,9 +19,9 @@
 
 ORDER = (
     ("A", 0), ("A", 1), ("A", 2), ("A", 3), ("B", 1), ("B", 0), ("C", 1), ("B", 2), ("C", 0), ("B", 3),
-    ("D", 1), ("D", 0), ("C", 2), ("D", 2), ("D", 3), ("C", 3), ("E", 1), ("E", 0), ("F", 0), ("F", 1),
-    ("E", 2), ("F", 2), ("E", 3), ("G", 1), ("G", 0), ("H", 1), ("H", 0), ("G", 2), ("H", 2), ("G", 3),
-    ("F", 3), ("H", 3), ("I", 1), ("J", 1), ("I", 0), ("I", 2), ("I", 3), ("J", 0), ("J", 3), ("J", 2),
+    ("D", 1), ("D", 0), ("C", 2), ("D", 2), ("C", 3), ("D", 3), ("E", 1), ("F", 1), ("E", 0), ("F", 0),
+    ("E", 2), ("E", 3), ("F", 2), ("G", 1), ("H", 1), ("G", 0), ("H", 0), ("G", 2), ("H", 2), ("H", 3),
+    ("G", 3), ("F", 3), ("I", 1), ("I", 0), ("J", 0), ("I", 2), ("J", 2), ("I", 3), ("J", 3), ("J", 1),
     ("K", 0), ("K", 1), ("K", 2), ("K", 3),
 )
 

time: 38.1 us -> 37.9 us (level)
  no operation moved by 1% of the time
where the time goes in v5:
time: 37.9 us
  Pallas kernels  36 us (95%)
  local copies, waits for them, and re-layouts  1.84 us (5%)
    pallas_call x1, Pallas kernels, on_device(): pl.pallas_call(functools.partial(kernel, CHUNKS), out_shape=jax.ShapeDtyp...  36 us
    unnamed x1, local copies, waits for them, and re-layouts  1.84 us

profile of v5, /device:TPU:32, one launch (start us, length us, event | category | flops | bytes accessed | tf_op | source)
XLA Modules:
  0.0 37.9 jit_solution(17271654022540041021)
XLA Ops:
  0.0 36.0 %merge.1 = f32[2,32,14336]{2,1,0:T(8,128)S(1)} custom-call(s32[1,2,2]{2,1,0:T(2,128)} %keep_hbm.1, bf16[1,2,32,14336]{3,2,1,0:T(8,128)(2,1)} %deltas_ref.1, bf16[2,32,14336]{2,1,0:T(8,128)(2,1)} %base_ref.1), custom_call_target="tpu_custom_call" | custom-call | tf_op jit(solution)/shard_map/merge/pallas_call | solution.py:283
  36.0 1.8 %copy.5 = f32[2,32,14336]{2,1,0:T(8,128)} copy(f32[2,32,14336]{2,1,0:T(8,128)S(1)} %merge.1) | data formatting | bytes 7340032
